TPU v7x, 32 devices: a whole 2x2x4 slice. The times are simulated.
32 devices in a mesh: seq: 4 (over y, core), tp: 8 (over z, x).
Axes of the slice: x: 2, y: 2, z: 4, core: 2. Of those that a mesh axis runs over, the one named last changes fastest.
Arguments:
- tokens: bfloat16 [2048, 4608], P(('seq', 'tp')), may hold values from -6 to 6
- norm_gain: float32 [4608], replicated, may hold values from 0.1 to 1.9
- query_weight: bfloat16 [4608, 4096], P(None, 'tp'), may hold values from -6 to 6
- key_matrix: bfloat16 [4608, 2048], P(None, 'tp'), may hold values from -0.09375 to 0.09375
- value_matrix: bfloat16 [4608, 2048], P(None, 'tp'), may hold values from -0.09375 to 0.09375
- output_grad: bfloat16 [2048, 4096], P('seq', 'tp'), may hold values from -3 to 3
Outputs:
- input_gradient: bfloat16 [2048, 4608], P(('seq', 'tp'))
All inputs are finite; a program needn't handle non-finite values.
Results may differ from a plain program's by a relative error of at most 0.014.
The roundings to bfloat16 on the way count: a program that leaves them out, or rounds other values in their place, can miss the bound.
Values may be sent and summed in bfloat16 or wider, within the bound.
A program may use at most 64 MiB of HBM per device.

v0:
```python
import functools
import types

import jax
import jax.numpy as jnp
from jax import lax
from jax.experimental import pallas as pl
from jax.experimental.pallas import tpu as pltpu
from jax.sharding import PartitionSpec as P

HEAD_SIZE = 128
WINDOW = 640


SCALE = 1.0 / 12.0
CAP = 50.0
EPS = 1e-06
VMEM_BYTES = 60 * 1024 * 1024
QUERY_ROWS = 128
TILE = 256


def ring_place(index, n):
    odd = index % 2
    return (1 - odd) * (index // 2) + odd * (n - 1 - index // 2)


def ring_device(place, n):
    place = (place + n) % n
    late = place // (n // 2)
    return (1 - late) * 2 * place + late * (2 * (n - 1 - place) + 1)


def chunks_of(direction, hop, last):
    return (direction, 1 - direction) if hop < last else (direction,)


def greet(neighbours):
    barrier = pltpu.get_barrier_semaphore()
    for neighbour in neighbours:
        pl.semaphore_signal(
            barrier, inc=1, device_id=neighbour, device_id_type=pl.DeviceIdType.MESH
        )
    pl.semaphore_wait(barrier, len(neighbours))


def remote(source, target, send_sem, recv_sem, device):
    return pltpu.make_async_remote_copy(
        src_ref=source,
        dst_ref=target,
        send_sem=send_sem,
        recv_sem=recv_sem,
        device_id=device,
        device_id_type=pl.DeviceIdType.MESH,
    )


def load_weights(weights, held, sems):
    copies = []
    start = 0
    for i, weight in enumerate(weights):
        cols = weight.shape[1]
        copies.append(
            pltpu.make_async_copy(weight, held.at[:, start : start + cols], sems.at[i])
        )
        start += cols
    for copy in copies:
        copy.start()
    return copies


def rows_at(index, count):
    return pl.ds(pl.multiple_of(index * count, count), count)


def gather_phase(n, ring, onward, tokens, gain, loads, s):
    rows, _ = tokens.shape
    local = n * rows
    half = rows // 2
    last = n // 2
    query_cols = s.query.shape[1]
    pair_cols = s.pairs.shape[1]
    me = lax.axis_index("tp")
    place = ring_place(me, n)
    sends = []
    halos = []

    def sender(direction, hop, chunk):
        step = -(hop - 1) if direction == 0 else hop - 1
        owner = ring_device(place + step, n)
        part = pl.ds(chunk * half, half)
        return remote(
            tokens.at[part] if hop == 1 else s.gathered.at[owner, part],
            s.gathered.at[owner, part],
            s.gather_send.at[direction, hop - 1, chunk],
            s.gather_recv.at[direction, hop - 1, chunk],
            ring[direction],
        )

    def project(sources):
        for i, (block, _) in enumerate(sources):
            values = block[...].astype(jnp.float32)
            scale = lax.rsqrt(jnp.mean(values * values, axis=1, keepdims=True) + EPS)
            s.normed[i * rows : (i + 1) * rows] = (values * scale * gain[...]).astype(jnp.bfloat16)
        count = len(sources) * rows

        def column(target, base, first):
            def write(j, carry):
                product = jnp.dot(
                    s.normed[:count],
                    s.held[:, pl.ds(pl.multiple_of(first + j * TILE, TILE), TILE)],
                    preferred_element_type=jnp.float32,
                ).astype(jnp.bfloat16)
                for i, (_, owner) in enumerate(sources):
                    at = pl.ds(pl.multiple_of(base + owner * rows, rows), rows)
                    target[at, rows_at(j, TILE)] = product[i * rows : (i + 1) * rows]
                return carry

            return write

        lax.fori_loop(0, pair_cols // TILE, column(s.pairs, 2 * local, query_cols), 0)
        for _, owner in sources:
            for back in range(2):
                source = pl.ds(pl.multiple_of(2 * local + owner * rows, rows), rows)
                target = pl.ds(pl.multiple_of((1 - back) * local + owner * rows, rows), rows)
                halos.append(
                    remote(
                        s.pairs.at[source],
                        s.pairs.at[target],
                        s.halo_send.at[back, len(halos) // 2],
                        s.halo_recv.at[back, len(halos) // 2],
                        onward[back],
                    )
                )
                halos[-1].start()
        lax.fori_loop(0, query_cols // TILE, column(s.query, 0, 0), 0)

    for position in range(2):
        for direction in range(2):
            order = chunks_of(direction, 1, last)
            if position < len(order):
                sends.append(sender(direction, 1, order[position]))
                sends[-1].start()
    for copy in loads:
        copy.wait()
    project([(tokens, me)])
    for hop in range(1, last + 1):
        for position in range(2):
            for direction in range(2):
                order = chunks_of(direction, hop, last)
                if position < len(order):
                    chunk = order[position]
                    sender(direction, hop, chunk).wait_recv()
                    if hop < last and chunk in chunks_of(direction, hop + 1, last):
                        sends.append(sender(direction, hop + 1, chunk))
                        sends[-1].start()
        owners = [ring_device(place - hop, n)]
        if hop < last:
            owners.append(ring_device(place + hop, n))
        project([(s.gathered.at[owner], owner) for owner in owners])
    for copy in halos:
        copy.wait_recv()
    return sends + halos


def dot(lhs, rhs, left, right):
    return lax.dot_general(
        lhs, rhs, (((left,), (right,)), ((), ())), preferred_element_type=jnp.float32
    )


def attention_phase(backward, output_grad, s, meanwhile):
    local, query_cols = s.query.shape
    key_cols = s.pairs.shape[1] // 2
    kv_heads = key_cols // HEAD_SIZE
    groups = query_cols // key_cols
    reach = WINDOW - local
    span = WINDOW + QUERY_ROWS
    start = 2 * local - WINDOW
    anchor = lax.axis_index("seq") * local
    shape = (span, groups * QUERY_ROWS)
    key_at = lax.broadcasted_iota(jnp.int32, shape, 0)
    gap = key_at - lax.broadcasted_iota(jnp.int32, shape, 1) % QUERY_ROWS
    s.band[...] = jnp.where((gap > 0) & (gap <= WINDOW), key_at, -1)
    s.sums[...] = jnp.zeros_like(s.sums)
    sends = []

    count = local // QUERY_ROWS
    late = (count - 1) * QUERY_ROWS
    pieces = (
        (0, reach, 1),
        (reach, late - QUERY_ROWS, 0),
        (late - QUERY_ROWS, late, 0),
        (late, WINDOW, 0),
    )
    stages = (
        ((0, count - 2), (0, 1)),
        ((count - 2, count - 1), (2,)),
        ((count - 1, count), (3,)),
    )

    def halo(head, piece):
        first, end, back = pieces[piece]
        part = pl.ds(first, end - first)
        return remote(
            s.leaving.at[head, part],
            s.arriving.at[head, part],
            s.back_send.at[head, piece],
            s.back_recv.at[head, piece],
            backward[back],
        )

    def head_block(head, i):
        key_lanes = slice(head * HEAD_SIZE, (head + 1) * HEAD_SIZE)
        value_lanes = slice(key_cols + head * HEAD_SIZE, key_cols + (head + 1) * HEAD_SIZE)
        heads = [
            slice((head * groups + g) * HEAD_SIZE, (head * groups + g + 1) * HEAD_SIZE)
            for g in range(groups)
        ]
        own = rows_at(i, QUERY_ROWS)
        seen = pl.ds(pl.multiple_of(start + i * QUERY_ROWS, QUERY_ROWS), span)
        query = jnp.concatenate([s.query[own, lanes] for lanes in heads], axis=0)
        grad = jnp.concatenate([output_grad[own, lanes] for lanes in heads], axis=0)
        key = s.pairs[seen, key_lanes]
        value = s.pairs[seen, value_lanes]
        bent = jnp.tanh(dot(key, query, 1, 1) * (SCALE / CAP))
        first = jnp.maximum(WINDOW - anchor - i * QUERY_ROWS, 0)
        expo = jnp.where(s.band[...] >= first, jnp.exp(CAP * bent), 0.0)
        probs = expo * (1.0 / jnp.sum(expo, axis=0, keepdims=True))
        d_probs = dot(value, grad, 1, 1)
        delta = jnp.sum(probs * d_probs, axis=0, keepdims=True)
        d_raw = (probs * (d_probs - delta) * (1.0 - bent * bent) * SCALE).astype(jnp.bfloat16)
        at = pl.ds(pl.multiple_of(i * QUERY_ROWS, QUERY_ROWS), span)
        s.sums[head, at, :HEAD_SIZE] += dot(d_raw, query, 1, 0)
        s.sums[head, at, HEAD_SIZE:] += dot(probs.astype(jnp.bfloat16), grad, 1, 0)
        grad_query = dot(d_raw, key, 0, 0).astype(jnp.bfloat16)
        for g, lanes in enumerate(heads):
            s.grads[own, lanes] = grad_query[g * QUERY_ROWS : (g + 1) * QUERY_ROWS]

    def block(i, carry):
        for head in range(kv_heads):
            head_block(head, i)
        return carry

    for blocks, ready in stages:
        lax.fori_loop(*blocks, block, 0)
        for head in range(kv_heads):
            for piece in ready:
                first, end, _ = pieces[piece]
                s.leaving[head, first:end] = s.sums[head, first:end].astype(jnp.bfloat16)
                sends.append(halo(head, piece))
                sends[-1].start()
    meanwhile()
    for head in range(kv_heads):
        for piece in range(len(pieces)):
            halo(head, piece).wait_recv()
        s.sums[head, WINDOW:] += s.arriving[head, reach:].astype(jnp.float32)
        s.sums[head, WINDOW + local - reach :] += s.arriving[head, :reach].astype(jnp.float32)
        for side in range(2):
            lanes = slice(side * HEAD_SIZE, (side + 1) * HEAD_SIZE)
            column = query_cols + side * key_cols + head * HEAD_SIZE
            s.grads[:, column : column + HEAD_SIZE] = s.sums[head, WINDOW:, lanes].astype(
                jnp.bfloat16
            )
    return sends


def farthest_query_sums(n, rows, s):
    query_cols = s.query.shape[1]
    place = ring_place(lax.axis_index("tp"), n)
    s.picked[:rows, :query_cols] = s.grads[
        rows_at(ring_device(place + n // 2, n), rows), :query_cols
    ]

    def column(j, carry):
        at = rows_at(j, TILE)
        s.total[:rows, at] = dot(s.picked[:rows, :query_cols], s.held[at, :query_cols], 1, 1)
        return carry

    lax.fori_loop(0, s.total.shape[1] // TILE, column, 0)


def scatter_phase(n, ring, tokens, gain, out, s):
    rows, width = tokens.shape
    half = rows // 2
    last = n // 2
    split = width // 2
    query_cols = s.query.shape[1]
    me = lax.axis_index("tp")
    place = ring_place(me, n)

    def sender(direction, hop, chunk):
        part = pl.ds(chunk * half, half)
        return remote(
            s.outgoing.at[direction, hop - 1, part],
            s.incoming.at[direction, hop - 1, part],
            s.scatter_send.at[direction, hop - 1, chunk],
            s.scatter_recv.at[direction, hop - 1, chunk],
            ring[direction],
        )

    def far_sender(direction, side):
        part = pl.ds(direction * half, half)
        lanes = pl.ds(side * split, split)
        return remote(
            s.outgoing.at[direction, last - 1, part, lanes],
            s.incoming.at[direction, last - 1, part, lanes],
            s.scatter_send.at[direction, last - 1, side],
            s.scatter_recv.at[direction, last - 1, side],
            ring[direction],
        )

    def partial_sums(owners):
        for i, owner in enumerate(owners):
            s.picked[i * rows : (i + 1) * rows] = s.grads[rows_at(owner, rows)]
        count = len(owners) * rows

        def column(j, carry):
            at = rows_at(j, TILE)
            s.total[:count, at] = dot(s.picked[:count], s.held[at, :], 1, 1)
            return carry

        lax.fori_loop(0, width // TILE, column, 0)

    def arrivals(direction, hop, chunk):
        if hop < last:
            sender(direction, hop, chunk).wait_recv()
        else:
            for side in range(2):
                far_sender(direction, side).wait_recv()

    sends = []
    s.picked[:rows] = s.grads[rows_at(ring_device(place + last, n), rows)]
    for side in range(2):

        def add_pairs(j, carry):
            at = rows_at(j, TILE)
            s.total[:rows, at] += dot(
                s.picked[:rows, query_cols:], s.held[at, query_cols:], 1, 1
            )
            return carry

        tiles = split // TILE
        lax.fori_loop(side * tiles, (side + 1) * tiles, add_pairs, 0)
        lanes = slice(side * split, (side + 1) * split)
        for direction in range(2):
            part = slice(direction * half, (direction + 1) * half)
            s.outgoing[direction, last - 1, part, lanes] = s.total[part, lanes].astype(jnp.bfloat16)
            sends.append(far_sender(direction, side))
            sends[-1].start()
    for hop in range(last - 1, 0, -1):
        partial_sums([ring_device(place + hop, n), ring_device(place - hop, n)])
        for position in (1, 0):
            for direction in range(2):
                order = chunks_of(direction, hop, last)
                if position < len(order):
                    chunk = order[position]
                    base = direction * rows
                    part = slice(chunk * half, (chunk + 1) * half)
                    value = s.total[base + chunk * half : base + (chunk + 1) * half]
                    if chunk in chunks_of(direction, hop + 1, last):
                        arrivals(direction, hop + 1, chunk)
                        value = value + s.incoming[direction, hop, part].astype(jnp.float32)
                    s.outgoing[direction, hop - 1, part] = value.astype(jnp.bfloat16)
                    sends.append(sender(direction, hop, chunk))
                    sends[-1].start()
    partial_sums([me])
    for chunk in (1, 0):
        part = slice(chunk * half, (chunk + 1) * half)
        value = s.total[part]
        for direction in range(2):
            if chunk in chunks_of(direction, 1, last):
                arrivals(direction, 1, chunk)
                value = value + s.incoming[direction, 0, part].astype(jnp.float32)
        values = tokens[part].astype(jnp.float32)
        scale = lax.rsqrt(jnp.mean(values * values, axis=1, keepdims=True) + EPS)
        upper = value * gain[...]
        unit = values * scale
        out[part] = (
            scale * (upper - unit * jnp.mean(upper * unit, axis=1, keepdims=True))
        ).astype(jnp.bfloat16)
    return sends


def kernel(names, n, seqs, tokens, gain_ref, output_grad, wq, wk, wv, out, *scratch):
    s = types.SimpleNamespace(**dict(zip(names, scratch)))
    gain = s.gain
    loads = load_weights((wq, wk, wv), s.held, s.load_sems)
    place = ring_place(lax.axis_index("tp"), n)
    block = lax.axis_index("seq")
    ring = [{"tp": ring_device(place + step, n)} for step in (1, -1)]
    onward = [{"seq": (block + step) % seqs} for step in (1, 2)]
    backward = [{"seq": (block + seqs - step) % seqs} for step in (1, 2)]
    gain[...] = gain_ref[...].reshape(gain.shape)
    greet(ring + onward + backward)
    sends = gather_phase(n, ring, onward, tokens, gain, loads, s)
    meanwhile = functools.partial(farthest_query_sums, n, tokens.shape[0], s)
    sends += attention_phase(backward, output_grad, s, meanwhile)
    sends += scatter_phase(n, ring, tokens, gain, out, s)
    for copy in sends:
        copy.wait_send()


def on_device(tokens, norm_gain, query_weight, key_matrix, value_matrix, output_grad):
    n = lax.axis_size("tp")
    rows, width = tokens.shape
    local, query_cols = output_grad.shape
    key_cols = key_matrix.shape[1]
    cols = query_cols + 2 * key_cols
    kv_heads = key_cols // HEAD_SIZE
    groups = query_cols // key_cols
    low, full = jnp.bfloat16, jnp.float32
    hops = pltpu.SemaphoreType.DMA((2, n // 2, 2))
    blocks = pltpu.SemaphoreType.DMA((2, n))
    heads = pltpu.SemaphoreType.DMA((kv_heads, 4))
    scratch = dict(
        gain=pltpu.VMEM((1, width), full),
        gathered=pltpu.VMEM((n, rows, width), low),
        held=pltpu.VMEM((width, cols), low),
        normed=pltpu.VMEM((2 * rows, width), low),
        query=pltpu.VMEM((local, query_cols), low),
        pairs=pltpu.VMEM((3 * local, 2 * key_cols), low),
        band=pltpu.VMEM((WINDOW + QUERY_ROWS, groups * QUERY_ROWS), jnp.int32),
        sums=pltpu.VMEM((kv_heads, WINDOW + local, 2 * HEAD_SIZE), full),
        leaving=pltpu.VMEM((kv_heads, WINDOW, 2 * HEAD_SIZE), low),
        arriving=pltpu.VMEM((kv_heads, WINDOW, 2 * HEAD_SIZE), low),
        grads=pltpu.VMEM((local, cols), low),
        outgoing=pltpu.VMEM((2, n // 2, rows, width), low),
        incoming=pltpu.VMEM((2, n // 2, rows, width), low),
        picked=pltpu.VMEM((2 * rows, cols), low),
        total=pltpu.VMEM((2 * rows, width), full),
        gather_send=hops,
        gather_recv=hops,
        halo_send=blocks,
        halo_recv=blocks,
        back_send=heads,
        back_recv=heads,
        scatter_send=hops,
        scatter_recv=hops,
        load_sems=pltpu.SemaphoreType.DMA((3,)),
    )
    vmem = pl.BlockSpec(memory_space=pltpu.VMEM)
    hbm = pl.BlockSpec(memory_space=pl.ANY)
    return pl.pallas_call(
        functools.partial(kernel, tuple(scratch), n, lax.axis_size("seq")),
        out_shape=jax.ShapeDtypeStruct((rows, width), low),
        in_specs=[vmem, vmem, vmem, hbm, hbm, hbm],
        out_specs=vmem,
        scratch_shapes=list(scratch.values()),
        compiler_params=pltpu.CompilerParams(
            collective_id=0, has_side_effects=True, vmem_limit_bytes=VMEM_BYTES
        ),
        name="attention_backward",
    )(tokens, norm_gain, output_grad, query_weight, key_matrix, value_matrix)


def solution(mesh):
    return jax.shard_map(
        on_device,
        mesh=mesh,
        in_specs=(
            P(("seq", "tp"), None),
            P(),
            P(None, "tp"),
            P(None, "tp"),
            P(None, "tp"),
            P("seq", "tp"),
        ),
        out_specs=P(("seq", "tp"), None),
        check_vma=False,
    )
```

profile of v0, /device:TPU:1, one launch (start us, length us, event | category | flops | bytes accessed | tf_op | source)
XLA Modules:
  0.0 123.1 jit_solution(59108547462020594)
XLA Ops:
  0.0 121.2 %attention_backward.1 = bf16[64,4608]{1,0:T(8,128)(2,1)} custom-call(bf16[64,4608]{1,0:T(8,128)(2,1)} %tokens.1, f32[4608]{0:T(1024)} %gain_ref.1, bf16[512,512]{1,0:T(8,128)(2,1)} %output_grad.1, bf16[4608,512]{1,0:T(8,128)(2,1)} %wq.1, bf16[4608,256]{1,0:T(8,128)(2,1)} %wk.1, bf16[4608,256]{1,0:T(8,128)(2,1)} %wv.1), custom_call_target="tpu_custom_call" | custom-call | tf_op jit(solution)/shard_map/attention_backward/pallas_call | solution.py:444
  121.2 1.9 %copy.8 = bf16[64,4608]{1,0:T(8,128)(2,1)} copy(bf16[64,4608]{1,0:T(8,128)(2,1)} %attention_backward.1) | data formatting | bytes 1179648
where the time goes:
time: 123 us
  Pallas kernels  121 us (98%)
  local copies, waits for them, and re-layouts  1.92 us (2%)
    pallas_call x1, Pallas kernels, on_device(): pl.pallas_call(functools.partial(kernel, tuple(scratch), n, lax.axis_size...  121 us

commit v1 on v0

--- a/solution.py
+++ b/solution.py
@@ -17,6 +17,8 @@
 EPS = 1e-06
 VMEM_BYTES = 60 * 1024 * 1024
 QUERY_ROWS = 128
+KEY_TILE = 256
+LOG2E = 1.4426950408889634
 TILE = 256
 
 
@@ -41,7 +43,17 @@
         pl.semaphore_signal(
             barrier, inc=1, device_id=neighbour, device_id_type=pl.DeviceIdType.MESH
         )
-    pl.semaphore_wait(barrier, len(neighbours))
+
+
+def hear(neighbours):
+    pl.semaphore_wait(pltpu.get_barrier_semaphore(), len(neighbours))
+
+
+def when(needed, act):
+    if needed is None:
+        act()
+    else:
+        pl.when(needed)(act)
 
 
 def remote(source, target, send_sem, recv_sem, device):
@@ -64,8 +76,6 @@
             pltpu.make_async_copy(weight, held.at[:, start : start + cols], sems.at[i])
         )
         start += cols
-    for copy in copies:
-        copy.start()
     return copies
 
 
@@ -123,16 +133,16 @@
             for back in range(2):
                 source = pl.ds(pl.multiple_of(2 * local + owner * rows, rows), rows)
                 target = pl.ds(pl.multiple_of((1 - back) * local + owner * rows, rows), rows)
-                halos.append(
-                    remote(
-                        s.pairs.at[source],
-                        s.pairs.at[target],
-                        s.halo_send.at[back, len(halos) // 2],
-                        s.halo_recv.at[back, len(halos) // 2],
-                        onward[back],
-                    )
+                copy = remote(
+                    s.pairs.at[source],
+                    s.pairs.at[target],
+                    s.halo_send.at[back, len(halos) // 2],
+                    s.halo_recv.at[back, len(halos) // 2],
+                    onward[back],
                 )
-                halos[-1].start()
+                needed = (owner + 1) * rows > 2 * local - WINDOW if back else None
+                halos.append((copy, needed))
+                when(needed, copy.start)
         lax.fori_loop(0, query_cols // TILE, column(s.query, 0, 0), 0)
 
     for position in range(2):
@@ -143,6 +153,7 @@
                 sends[-1].start()
     for copy in loads:
         copy.wait()
+    gain[...] = s.gain_flat[...].reshape(gain.shape)
     project([(tokens, me)])
     for hop in range(1, last + 1):
         for position in range(2):
@@ -158,9 +169,9 @@
         if hop < last:
             owners.append(ring_device(place + hop, n))
         project([(s.gathered.at[owner], owner) for owner in owners])
-    for copy in halos:
-        copy.wait_recv()
-    return sends + halos
+    for copy, needed in halos:
+        when(needed, copy.wait_recv)
+    return [(copy, None) for copy in sends] + halos
 
 
 def dot(lhs, rhs, left, right):
@@ -178,84 +189,111 @@
     span = WINDOW + QUERY_ROWS
     start = 2 * local - WINDOW
     anchor = lax.axis_index("seq") * local
-    shape = (span, groups * QUERY_ROWS)
-    key_at = lax.broadcasted_iota(jnp.int32, shape, 0)
-    gap = key_at - lax.broadcasted_iota(jnp.int32, shape, 1) % QUERY_ROWS
-    s.band[...] = jnp.where((gap > 0) & (gap <= WINDOW), key_at, -1)
+    shape = (QUERY_ROWS, groups * QUERY_ROWS)
+    s.gap[...] = lax.broadcasted_iota(jnp.int32, shape, 0) - (
+        lax.broadcasted_iota(jnp.int32, shape, 1) % QUERY_ROWS
+    )
     s.sums[...] = jnp.zeros_like(s.sums)
     sends = []
 
     count = local // QUERY_ROWS
     late = (count - 1) * QUERY_ROWS
-    pieces = (
-        (0, reach, 1),
-        (reach, late - QUERY_ROWS, 0),
-        (late - QUERY_ROWS, late, 0),
-        (late, WINDOW, 0),
-    )
-    stages = (
-        ((0, count - 2), (0, 1)),
-        ((count - 2, count - 1), (2,)),
-        ((count - 1, count), (3,)),
-    )
-
-    def halo(head, piece):
-        first, end, back = pieces[piece]
-        part = pl.ds(first, end - first)
+
+    def halo(head, piece, rows):
+        part = pl.ds(pl.multiple_of(piece * QUERY_ROWS, QUERY_ROWS), rows)
         return remote(
             s.leaving.at[head, part],
             s.arriving.at[head, part],
             s.back_send.at[head, piece],
             s.back_recv.at[head, piece],
-            backward[back],
+            backward,
         )
 
-    def head_block(head, i):
-        key_lanes = slice(head * HEAD_SIZE, (head + 1) * HEAD_SIZE)
-        value_lanes = slice(key_cols + head * HEAD_SIZE, key_cols + (head + 1) * HEAD_SIZE)
-        heads = [
+    def send_back(head, piece, rows):
+        part = pl.ds(pl.multiple_of(piece * QUERY_ROWS, QUERY_ROWS), rows)
+        s.leaving[head, part] = s.sums[head, part].astype(jnp.bfloat16)
+        halo(head, piece, rows).start()
+
+    def lanes_of(head):
+        return [
             slice((head * groups + g) * HEAD_SIZE, (head * groups + g + 1) * HEAD_SIZE)
             for g in range(groups)
         ]
-        own = rows_at(i, QUERY_ROWS)
-        seen = pl.ds(pl.multiple_of(start + i * QUERY_ROWS, QUERY_ROWS), span)
-        query = jnp.concatenate([s.query[own, lanes] for lanes in heads], axis=0)
-        grad = jnp.concatenate([output_grad[own, lanes] for lanes in heads], axis=0)
-        key = s.pairs[seen, key_lanes]
-        value = s.pairs[seen, value_lanes]
-        bent = jnp.tanh(dot(key, query, 1, 1) * (SCALE / CAP))
-        first = jnp.maximum(WINDOW - anchor - i * QUERY_ROWS, 0)
-        expo = jnp.where(s.band[...] >= first, jnp.exp(CAP * bent), 0.0)
-        probs = expo * (1.0 / jnp.sum(expo, axis=0, keepdims=True))
-        d_probs = dot(value, grad, 1, 1)
-        delta = jnp.sum(probs * d_probs, axis=0, keepdims=True)
-        d_raw = (probs * (d_probs - delta) * (1.0 - bent * bent) * SCALE).astype(jnp.bfloat16)
-        at = pl.ds(pl.multiple_of(i * QUERY_ROWS, QUERY_ROWS), span)
-        s.sums[head, at, :HEAD_SIZE] += dot(d_raw, query, 1, 0)
-        s.sums[head, at, HEAD_SIZE:] += dot(probs.astype(jnp.bfloat16), grad, 1, 0)
-        grad_query = dot(d_raw, key, 0, 0).astype(jnp.bfloat16)
-        for g, lanes in enumerate(heads):
-            s.grads[own, lanes] = grad_query[g * QUERY_ROWS : (g + 1) * QUERY_ROWS]
-
-    def block(i, carry):
-        for head in range(kv_heads):
-            head_block(head, i)
-        return carry
-
-    for blocks, ready in stages:
-        lax.fori_loop(*blocks, block, 0)
-        for head in range(kv_heads):
-            for piece in ready:
-                first, end, _ = pieces[piece]
-                s.leaving[head, first:end] = s.sums[head, first:end].astype(jnp.bfloat16)
-                sends.append(halo(head, piece))
-                sends[-1].start()
+
+    def rows_of(ref, head, i):
+        own = slice(i * QUERY_ROWS, (i + 1) * QUERY_ROWS)
+        return jnp.concatenate([ref[own, lanes] for lanes in lanes_of(head)], axis=0)
+
+    def seen_by(head, i, tile, base):
+        rows = slice(start + i * QUERY_ROWS + tile, start + i * QUERY_ROWS + tile + KEY_TILE)
+        return s.pairs[rows, base + head * HEAD_SIZE : base + (head + 1) * HEAD_SIZE]
+
+    def scores(head, i, slot):
+        query = rows_of(s.query, head, i)
+        grad = rows_of(output_grad, head, i)
+        first = WINDOW - anchor - i * QUERY_ROWS
+        total = jnp.zeros((8, shape[1]), jnp.float32)
+        along = jnp.zeros((8, shape[1]), jnp.float32)
+        for tile in range(0, span, KEY_TILE):
+            bent_tile = jnp.tanh(dot(seen_by(head, i, tile, 0), query, 1, 1) * (SCALE / CAP))
+            d_tile = dot(seen_by(head, i, tile, key_cols), grad, 1, 1)
+            for part in range(0, KEY_TILE, QUERY_ROWS):
+                row = tile + part
+                bent = bent_tile[part : part + QUERY_ROWS]
+                d_probs = d_tile[part : part + QUERY_ROWS]
+                expo = jnp.exp2(bent * (CAP * LOG2E))
+                if row == 0:
+                    expo = jnp.where(s.gap[...] > jnp.where(first > 0, QUERY_ROWS, 0), expo, 0.0)
+                elif row < WINDOW:
+                    expo = expo * jnp.where(first > row, 0.0, 1.0)
+                else:
+                    expo = jnp.where(s.gap[...] <= 0, expo, 0.0)
+                total += jnp.sum(expo.reshape(-1, 8, shape[1]), axis=0)
+                along += jnp.sum((expo * d_probs).reshape(-1, 8, shape[1]), axis=0)
+                at = slice(row, row + QUERY_ROWS)
+                s.expo[slot, at] = expo.astype(jnp.bfloat16)
+                s.slope[slot, at] = expo * (1.0 - bent * bent)
+                s.d_probs[slot, at] = d_probs
+        inverse = 1.0 / jnp.sum(total, axis=0, keepdims=True)
+        delta = jnp.sum(along, axis=0, keepdims=True) * inverse
+        column = jnp.transpose(jnp.broadcast_to(inverse, shape))
+        return inverse, delta, column
+
+    def gradients(head, i, slot, inverse, delta, column):
+        query = (rows_of(s.query, head, i).astype(jnp.float32) * (column * SCALE)).astype(jnp.bfloat16)
+        grad = (rows_of(output_grad, head, i).astype(jnp.float32) * column).astype(jnp.bfloat16)
+        grad_query = jnp.zeros((shape[1], HEAD_SIZE), jnp.float32)
+        for tile in range(0, span, KEY_TILE):
+            rows = slice(tile, tile + KEY_TILE)
+            d_raw = (s.slope[slot, rows] * (s.d_probs[slot, rows] - delta)).astype(jnp.bfloat16)
+            at = slice(i * QUERY_ROWS + tile, i * QUERY_ROWS + tile + KEY_TILE)
+            s.sums[head, at, :HEAD_SIZE] += dot(d_raw, query, 1, 0)
+            s.sums[head, at, HEAD_SIZE:] += dot(s.expo[slot, rows], grad, 1, 0)
+            grad_query += dot(d_raw, seen_by(head, i, tile, 0), 0, 0)
+        grad_query = (grad_query * (column * SCALE)).astype(jnp.bfloat16)
+        for g, lanes in enumerate(lanes_of(head)):
+            s.grads[i * QUERY_ROWS : (i + 1) * QUERY_ROWS, lanes] = grad_query[
+                g * QUERY_ROWS : (g + 1) * QUERY_ROWS
+            ]
+
+    pieces = [(piece, QUERY_ROWS) for piece in range(count - 1)] + [(count - 1, WINDOW - late)]
+    steps = [(head, i) for head in range(kv_heads) for i in range(count)]
+    ready = scores(*steps[0], 0)
+    for k, (head, i) in enumerate(steps):
+        now = ready
+        if k + 1 < len(steps):
+            ready = scores(*steps[k + 1], (k + 1) % 2)
+        gradients(head, i, k % 2, *now)
+        if i + 1 == count:
+            halo(head, 0, QUERY_ROWS).wait_recv()
+            s.sums[head, local:WINDOW] += s.arriving[head, :reach].astype(jnp.float32)
+        send_back(head, *pieces[i])
+        sends.append((halo(head, *pieces[i]), None))
     meanwhile()
     for head in range(kv_heads):
-        for piece in range(len(pieces)):
-            halo(head, piece).wait_recv()
+        for piece in pieces[1:]:
+            halo(head, *piece).wait_recv()
         s.sums[head, WINDOW:] += s.arriving[head, reach:].astype(jnp.float32)
-        s.sums[head, WINDOW + local - reach :] += s.arriving[head, :reach].astype(jnp.float32)
         for side in range(2):
             lanes = slice(side * HEAD_SIZE, (side + 1) * HEAD_SIZE)
             column = query_cols + side * key_cols + head * HEAD_SIZE
@@ -382,23 +420,29 @@
     return sends
 
 
-def kernel(names, n, seqs, tokens, gain_ref, output_grad, wq, wk, wv, out, *scratch):
+def kernel(names, n, seqs, tokens_ref, gain_ref, grad_ref, wq, wk, wv, out, *scratch):
     s = types.SimpleNamespace(**dict(zip(names, scratch)))
-    gain = s.gain
-    loads = load_weights((wq, wk, wv), s.held, s.load_sems)
     place = ring_place(lax.axis_index("tp"), n)
     block = lax.axis_index("seq")
     ring = [{"tp": ring_device(place + step, n)} for step in (1, -1)]
     onward = [{"seq": (block + step) % seqs} for step in (1, 2)]
     backward = [{"seq": (block + seqs - step) % seqs} for step in (1, 2)]
-    gain[...] = gain_ref[...].reshape(gain.shape)
     greet(ring + onward + backward)
-    sends = gather_phase(n, ring, onward, tokens, gain, loads, s)
+    tokens = s.tokens
+    load = pltpu.make_async_copy(tokens_ref, tokens, s.load_sems.at[3])
+    loads = load_weights((wq, wk, wv), s.held, s.load_sems)
+    loads.append(pltpu.make_async_copy(gain_ref, s.gain_flat, s.load_sems.at[4]))
+    loads.append(pltpu.make_async_copy(grad_ref, s.output_grad, s.load_sems.at[5]))
+    for copy in [load] + loads:
+        copy.start()
+    load.wait()
+    hear(ring + onward + backward)
+    sends = gather_phase(n, ring, onward, tokens, s.gain, loads, s)
     meanwhile = functools.partial(farthest_query_sums, n, tokens.shape[0], s)
-    sends += attention_phase(backward, output_grad, s, meanwhile)
-    sends += scatter_phase(n, ring, tokens, gain, out, s)
-    for copy in sends:
-        copy.wait_send()
+    sends += attention_phase(backward[0], s.output_grad, s, meanwhile)
+    sends += [(copy, None) for copy in scatter_phase(n, ring, tokens, s.gain, out, s)]
+    for copy, needed in sends:
+        when(needed, copy.wait_send)
 
 
 def on_device(tokens, norm_gain, query_weight, key_matrix, value_matrix, output_grad):
@@ -412,15 +456,21 @@
     low, full = jnp.bfloat16, jnp.float32
     hops = pltpu.SemaphoreType.DMA((2, n // 2, 2))
     blocks = pltpu.SemaphoreType.DMA((2, n))
-    heads = pltpu.SemaphoreType.DMA((kv_heads, 4))
+    heads = pltpu.SemaphoreType.DMA((kv_heads, local // QUERY_ROWS))
     scratch = dict(
+        tokens=pltpu.VMEM((rows, width), low),
+        output_grad=pltpu.VMEM((local, query_cols), low),
+        gain_flat=pltpu.VMEM((width,), full),
         gain=pltpu.VMEM((1, width), full),
         gathered=pltpu.VMEM((n, rows, width), low),
         held=pltpu.VMEM((width, cols), low),
         normed=pltpu.VMEM((2 * rows, width), low),
         query=pltpu.VMEM((local, query_cols), low),
         pairs=pltpu.VMEM((3 * local, 2 * key_cols), low),
-        band=pltpu.VMEM((WINDOW + QUERY_ROWS, groups * QUERY_ROWS), jnp.int32),
+        gap=pltpu.VMEM((QUERY_ROWS, groups * QUERY_ROWS), jnp.int32),
+        expo=pltpu.VMEM((2, WINDOW + QUERY_ROWS, groups * QUERY_ROWS), low),
+        slope=pltpu.VMEM((2, WINDOW + QUERY_ROWS, groups * QUERY_ROWS), full),
+        d_probs=pltpu.VMEM((2, WINDOW + QUERY_ROWS, groups * QUERY_ROWS), full),
         sums=pltpu.VMEM((kv_heads, WINDOW + local, 2 * HEAD_SIZE), full),
         leaving=pltpu.VMEM((kv_heads, WINDOW, 2 * HEAD_SIZE), low),
         arriving=pltpu.VMEM((kv_heads, WINDOW, 2 * HEAD_SIZE), low),
@@ -437,14 +487,14 @@
         back_recv=heads,
         scatter_send=hops,
         scatter_recv=hops,
-        load_sems=pltpu.SemaphoreType.DMA((3,)),
+        load_sems=pltpu.SemaphoreType.DMA((6,)),
     )
     vmem = pl.BlockSpec(memory_space=pltpu.VMEM)
     hbm = pl.BlockSpec(memory_space=pl.ANY)
     return pl.pallas_call(
         functools.partial(kernel, tuple(scratch), n, lax.axis_size("seq")),
-        out_shape=jax.ShapeDtypeStruct((rows, width), low),
-        in_specs=[vmem, vmem, vmem, hbm, hbm, hbm],
+        out_shape=pltpu.VMEM((rows, width), low),
+        in_specs=[hbm] * 6,
         out_specs=vmem,
         scratch_shapes=list(scratch.values()),
         compiler_params=pltpu.CompilerParams(

time: 123 us -> 118 us (0.959)
  Pallas kernels: 121 us -> 117 us
    pallas_call x1, Pallas kernels: 121 us -> 117 us  [on_device(): pl.pallas_call(functools.partial(kernel, tuple(scratch), n, lax.axis_size...]
where the time goes in v1:
time: 118 us
  Pallas kernels  117 us (99%)
    pallas_call x1, Pallas kernels, on_device(): pl.pallas_call(functools.partial(kernel, tuple(scratch), n, lax.axis_size...  117 us

profile of v1, /device:TPU:1, one launch (start us, length us, event | category | flops | bytes accessed | tf_op | source)
XLA Modules:
  0.0 117.7 jit_solution(15521929102366714495)
XLA Ops:
  0.0 116.9 %attention_backward.1 = bf16[64,4608]{1,0:T(8,128)(2,1)S(1)} custom-call(bf16[64,4608]{1,0:T(8,128)(2,1)} %tokens_ref.1, f32[4608]{0:T(1024)} %gain_ref.1, bf16[512,512]{1,0:T(8,128)(2,1)} %grad_ref.1, bf16[4608,512]{1,0:T(8,128)(2,1)} %wq.1, bf16[4608,256]{1,0:T(8,128)(2,1)} %wk.1, bf16[4608,256]{1,0:T(8,128)(2,1)} %wv.1), custom_call_target="tpu_custom_call" | custom-call | tf_op jit(solution)/shard_map/attention_backward/pallas_call | solution.py:494
  116.9 0.8 copy.8

commit v2 on v1

--- a/solution.py
+++ b/solution.py
@@ -18,6 +18,7 @@
 VMEM_BYTES = 60 * 1024 * 1024
 QUERY_ROWS = 128
 KEY_TILE = 256
+PIECES = 6
 LOG2E = 1.4426950408889634
 TILE = 256
 
@@ -303,121 +304,137 @@
     return sends
 
 
-def farthest_query_sums(n, rows, s):
-    query_cols = s.query.shape[1]
+def first_owners(n):
     place = ring_place(lax.axis_index("tp"), n)
-    s.picked[:rows, :query_cols] = s.grads[
-        rows_at(ring_device(place + n // 2, n), rows), :query_cols
-    ]
-
-    def column(j, carry):
-        at = rows_at(j, TILE)
-        s.total[:rows, at] = dot(s.picked[:rows, :query_cols], s.held[at, :query_cols], 1, 1)
+    steps = (n // 2, n // 2 - 1, 1 - n // 2)
+    return [ring_device(place + step, n) for step in steps]
+
+
+def later_owners(n):
+    place = ring_place(lax.axis_index("tp"), n)
+    steps = [step * hop for hop in range(n // 2 - 2, 0, -1) for step in (1, -1)]
+    return [ring_device(place + step, n) for step in steps + [0]]
+
+
+def pick(target, source, owners, rows, lanes):
+    for i, owner in enumerate(owners):
+        target[i * rows : (i + 1) * rows, lanes] = source[rows_at(owner, rows), lanes]
+
+
+def products(total, picked, s, lanes, piece, add):
+    count, width = total.shape[1:]
+    for j in range(0, width, TILE):
+        at = pl.ds(pl.multiple_of(piece * width + j, TILE), TILE)
+        product = dot(picked[:count, lanes], s.held[at, lanes], 1, 1)
+        if add:
+            product += total[piece, :, j : j + TILE]
+        total[piece, :, j : j + TILE] = product
+
+
+def first_query_sums(n, rows, s):
+    lanes = slice(0, s.query.shape[1])
+    pick(s.picked_first, s.grads, first_owners(n), rows, lanes)
+
+    def piece_sums(piece, carry):
+        products(s.first, s.picked_first, s, lanes, piece, False)
         return carry
 
-    lax.fori_loop(0, s.total.shape[1] // TILE, column, 0)
+    lax.fori_loop(0, PIECES, piece_sums, 0)
 
 
 def scatter_phase(n, ring, tokens, gain, out, s):
     rows, width = tokens.shape
-    half = rows // 2
     last = n // 2
-    split = width // 2
+    half = PIECES // 2
+    size = width // PIECES
+    cols = s.grads.shape[1]
     query_cols = s.query.shape[1]
-    me = lax.axis_index("tp")
-    place = ring_place(me, n)
-
-    def sender(direction, hop, chunk):
-        part = pl.ds(chunk * half, half)
+    far = [list(range(half)), list(range(half, PIECES))]
+    orders = [far[1] + far[0], far[0] + far[1]]
+
+    def sender(direction, hop, piece):
         return remote(
-            s.outgoing.at[direction, hop - 1, part],
-            s.incoming.at[direction, hop - 1, part],
-            s.scatter_send.at[direction, hop - 1, chunk],
-            s.scatter_recv.at[direction, hop - 1, chunk],
+            s.outgoing.at[direction, hop - 1, piece],
+            s.incoming.at[direction, hop - 1, piece],
+            s.scatter_send.at[direction, hop - 1, piece],
+            s.scatter_recv.at[direction, hop - 1, piece],
             ring[direction],
         )
 
-    def far_sender(direction, side):
-        part = pl.ds(direction * half, half)
-        lanes = pl.ds(side * split, split)
-        return remote(
-            s.outgoing.at[direction, last - 1, part, lanes],
-            s.incoming.at[direction, last - 1, part, lanes],
-            s.scatter_send.at[direction, last - 1, side],
-            s.scatter_recv.at[direction, last - 1, side],
-            ring[direction],
-        )
-
-    def partial_sums(owners):
-        for i, owner in enumerate(owners):
-            s.picked[i * rows : (i + 1) * rows] = s.grads[rows_at(owner, rows)]
-        count = len(owners) * rows
-
-        def column(j, carry):
-            at = rows_at(j, TILE)
-            s.total[:count, at] = dot(s.picked[:count], s.held[at, :], 1, 1)
-            return carry
-
-        lax.fori_loop(0, width // TILE, column, 0)
-
-    def arrivals(direction, hop, chunk):
-        if hop < last:
-            sender(direction, hop, chunk).wait_recv()
-        else:
-            for side in range(2):
-                far_sender(direction, side).wait_recv()
-
-    sends = []
-    s.picked[:rows] = s.grads[rows_at(ring_device(place + last, n), rows)]
-    for side in range(2):
-
-        def add_pairs(j, carry):
-            at = rows_at(j, TILE)
-            s.total[:rows, at] += dot(
-                s.picked[:rows, query_cols:], s.held[at, query_cols:], 1, 1
-            )
-            return carry
-
-        tiles = split // TILE
-        lax.fori_loop(side * tiles, (side + 1) * tiles, add_pairs, 0)
-        lanes = slice(side * split, (side + 1) * split)
+    def give(direction, hop, piece, value):
+        s.outgoing[direction, hop - 1, piece] = value.astype(jnp.bfloat16)
+        sender(direction, hop, piece).start()
+
+    def take(direction, hop, piece):
+        sender(direction, hop, piece).wait_recv()
+        return s.incoming[direction, hop - 1, piece].astype(jnp.float32)
+
+    lanes = slice(query_cols, cols)
+    pick(s.picked_first, s.grads, first_owners(n), rows, lanes)
+
+    def first_pair(k, carry):
         for direction in range(2):
-            part = slice(direction * half, (direction + 1) * half)
-            s.outgoing[direction, last - 1, part, lanes] = s.total[part, lanes].astype(jnp.bfloat16)
-            sends.append(far_sender(direction, side))
-            sends[-1].start()
-    for hop in range(last - 1, 0, -1):
-        partial_sums([ring_device(place + hop, n), ring_device(place - hop, n)])
-        for position in (1, 0):
+            piece = direction * half + k
+            products(s.first, s.picked_first, s, lanes, piece, True)
+            other = 1 - direction
+            block = (1 + other) * rows
+            give(direction, last, piece, s.first[piece, :rows])
+            give(other, last - 1, piece, s.first[piece, block : block + rows])
+        return carry
+
+    lax.fori_loop(0, half, first_pair, 0)
+    owners = later_owners(n)
+    pick(s.picked_later, s.grads, owners, rows, slice(0, cols))
+
+    def later_sums(piece, carry):
+        products(s.later, s.picked_later, s, slice(0, cols), piece, False)
+        return carry
+
+    lax.fori_loop(0, PIECES, later_sums, 0)
+    values = tokens[...].astype(jnp.float32)
+    scale = lax.rsqrt(jnp.mean(values * values, axis=1, keepdims=True) + EPS)
+    s.unit[...] = values * scale
+
+    for k in range(half):
+        for direction in range(2):
+            piece = far[direction][k]
+            block = (1 + direction) * rows
+            value = s.first[piece, block : block + rows]
+            give(direction, last - 1, piece, value + take(direction, last, piece))
+    for hop in range(last - 2, 0, -1):
+        for k in range(PIECES):
             for direction in range(2):
-                order = chunks_of(direction, hop, last)
-                if position < len(order):
-                    chunk = order[position]
-                    base = direction * rows
-                    part = slice(chunk * half, (chunk + 1) * half)
-                    value = s.total[base + chunk * half : base + (chunk + 1) * half]
-                    if chunk in chunks_of(direction, hop + 1, last):
-                        arrivals(direction, hop + 1, chunk)
-                        value = value + s.incoming[direction, hop, part].astype(jnp.float32)
-                    s.outgoing[direction, hop - 1, part] = value.astype(jnp.bfloat16)
-                    sends.append(sender(direction, hop, chunk))
-                    sends[-1].start()
-    partial_sums([me])
-    for chunk in (1, 0):
-        part = slice(chunk * half, (chunk + 1) * half)
-        value = s.total[part]
+                piece = orders[direction][k]
+                block = (2 * (last - 2 - hop) + direction) * rows
+                value = s.later[piece, block : block + rows]
+                give(direction, hop, piece, value + take(direction, hop + 1, piece))
+    along = jnp.zeros((rows, HEAD_SIZE), jnp.float32)
+    block = 2 * (last - 2) * rows
+    done = [set(), set()]
+    for k in range(PIECES):
         for direction in range(2):
-            if chunk in chunks_of(direction, 1, last):
-                arrivals(direction, 1, chunk)
-                value = value + s.incoming[direction, 0, part].astype(jnp.float32)
-        values = tokens[part].astype(jnp.float32)
-        scale = lax.rsqrt(jnp.mean(values * values, axis=1, keepdims=True) + EPS)
-        upper = value * gain[...]
-        unit = values * scale
-        out[part] = (
-            scale * (upper - unit * jnp.mean(upper * unit, axis=1, keepdims=True))
-        ).astype(jnp.bfloat16)
-    return sends
+            done[direction].add(orders[direction][k])
+        for piece in sorted(done[0] & done[1]):
+            for direction in range(2):
+                done[direction].remove(piece)
+            at = slice(piece * size, (piece + 1) * size)
+            value = s.later[piece, block : block + rows]
+            value = value + take(0, 1, piece) + take(1, 1, piece)
+            upper = value * gain[:, at]
+            s.upper[:, at] = upper
+            product = upper * s.unit[:, at]
+            for j in range(0, size, HEAD_SIZE):
+                along += product[:, j : j + HEAD_SIZE]
+    mean = jnp.sum(along, axis=1, keepdims=True) * (1.0 / width)
+    for piece in range(PIECES):
+        at = slice(piece * size, (piece + 1) * size)
+        out[:, at] = (scale * (s.upper[:, at] - s.unit[:, at] * mean)).astype(jnp.bfloat16)
+    return [
+        sender(direction, hop, piece)
+        for hop in range(last, 0, -1)
+        for direction in range(2)
+        for piece in (far[direction] if hop == last else orders[direction])
+    ]
 
 
 def kernel(names, n, seqs, tokens_ref, gain_ref, grad_ref, wq, wk, wv, out, *scratch):
@@ -438,7 +455,7 @@
     load.wait()
     hear(ring + onward + backward)
     sends = gather_phase(n, ring, onward, tokens, s.gain, loads, s)
-    meanwhile = functools.partial(farthest_query_sums, n, tokens.shape[0], s)
+    meanwhile = functools.partial(first_query_sums, n, tokens.shape[0], s)
     sends += attention_phase(backward[0], s.output_grad, s, meanwhile)
     sends += [(copy, None) for copy in scatter_phase(n, ring, tokens, s.gain, out, s)]
     for copy, needed in sends:
@@ -455,6 +472,7 @@
     groups = query_cols // key_cols
     low, full = jnp.bfloat16, jnp.float32
     hops = pltpu.SemaphoreType.DMA((2, n // 2, 2))
+    pieces = pltpu.SemaphoreType.DMA((2, n // 2, PIECES))
     blocks = pltpu.SemaphoreType.DMA((2, n))
     heads = pltpu.SemaphoreType.DMA((kv_heads, local // QUERY_ROWS))
     scratch = dict(
@@ -475,18 +493,22 @@
         leaving=pltpu.VMEM((kv_heads, WINDOW, 2 * HEAD_SIZE), low),
         arriving=pltpu.VMEM((kv_heads, WINDOW, 2 * HEAD_SIZE), low),
         grads=pltpu.VMEM((local, cols), low),
-        outgoing=pltpu.VMEM((2, n // 2, rows, width), low),
-        incoming=pltpu.VMEM((2, n // 2, rows, width), low),
-        picked=pltpu.VMEM((2 * rows, cols), low),
-        total=pltpu.VMEM((2 * rows, width), full),
+        outgoing=pltpu.VMEM((2, n // 2, PIECES, rows, width // PIECES), low),
+        incoming=pltpu.VMEM((2, n // 2, PIECES, rows, width // PIECES), low),
+        picked_first=pltpu.VMEM((3 * rows, cols), low),
+        picked_later=pltpu.VMEM(((n - 3) * rows, cols), low),
+        first=pltpu.VMEM((PIECES, 3 * rows, width // PIECES), full),
+        later=pltpu.VMEM((PIECES, (n - 3) * rows, width // PIECES), full),
+        unit=pltpu.VMEM((rows, width), full),
+        upper=pltpu.VMEM((rows, width), full),
         gather_send=hops,
         gather_recv=hops,
         halo_send=blocks,
         halo_recv=blocks,
         back_send=heads,
         back_recv=heads,
-        scatter_send=hops,
-        scatter_recv=hops,
+        scatter_send=pieces,
+        scatter_recv=pieces,
         load_sems=pltpu.SemaphoreType.DMA((6,)),
     )
     vmem = pl.BlockSpec(memory_space=pltpu.VMEM)

time: 118 us -> 114 us (0.966)
  Pallas kernels: 117 us -> 113 us
    pallas_call x1, Pallas kernels: 117 us -> 113 us  [on_device(): pl.pallas_call(functools.partial(kernel, tuple(scratch), n, lax.axis_size...]
where the time goes in v2:
time: 114 us
  Pallas kernels  113 us (99%)
    pallas_call x1, Pallas kernels, on_device(): pl.pallas_call(functools.partial(kernel, tuple(scratch), n, lax.axis_size...  113 us

profile of v2, /device:TPU:1, one launch (start us, length us, event | category | flops | bytes accessed | tf_op | source)
XLA Modules:
  0.0 114.3 jit_solution(10935021386768783256)
XLA Ops:
  0.0 113.5 %attention_backward.1 = bf16[64,4608]{1,0:T(8,128)(2,1)S(1)} custom-call(bf16[64,4608]{1,0:T(8,128)(2,1)} %tokens_ref.1, f32[4608]{0:T(1024)} %gain_ref.1, bf16[512,512]{1,0:T(8,128)(2,1)} %grad_ref.1, bf16[4608,512]{1,0:T(8,128)(2,1)} %wq.1, bf16[4608,256]{1,0:T(8,128)(2,1)} %wk.1, bf16[4608,256]{1,0:T(8,128)(2,1)} %wv.1), custom_call_target="tpu_custom_call" | custom-call | tf_op jit(solution)/shard_map/attention_backward/pallas_call | solution.py:516
  113.5 0.8 copy.8

commit v3 on v2

--- a/solution.py
+++ b/solution.py
@@ -156,6 +156,7 @@
         copy.wait()
     gain[...] = s.gain_flat[...].reshape(gain.shape)
     project([(tokens, me)])
+    prepare_attention(s)
     for hop in range(1, last + 1):
         for position in range(2):
             for direction in range(2):
@@ -181,7 +182,15 @@
     )
 
 
-def attention_phase(backward, output_grad, s, meanwhile):
+def prepare_attention(s):
+    shape = s.gap.shape
+    s.gap[...] = lax.broadcasted_iota(jnp.int32, shape, 0) - (
+        lax.broadcasted_iota(jnp.int32, shape, 1) % QUERY_ROWS
+    )
+    s.sums[...] = jnp.zeros_like(s.sums)
+
+
+def attention_phase(n, rows, backward, output_grad, s):
     local, query_cols = s.query.shape
     key_cols = s.pairs.shape[1] // 2
     kv_heads = key_cols // HEAD_SIZE
@@ -190,11 +199,7 @@
     span = WINDOW + QUERY_ROWS
     start = 2 * local - WINDOW
     anchor = lax.axis_index("seq") * local
-    shape = (QUERY_ROWS, groups * QUERY_ROWS)
-    s.gap[...] = lax.broadcasted_iota(jnp.int32, shape, 0) - (
-        lax.broadcasted_iota(jnp.int32, shape, 1) % QUERY_ROWS
-    )
-    s.sums[...] = jnp.zeros_like(s.sums)
+    shape = s.gap.shape
     sends = []
 
     count = local // QUERY_ROWS
@@ -278,7 +283,7 @@
             ]
 
     pieces = [(piece, QUERY_ROWS) for piece in range(count - 1)] + [(count - 1, WINDOW - late)]
-    steps = [(head, i) for head in range(kv_heads) for i in range(count)]
+    steps = [(head, i) for i in range(count) for head in range(kv_heads)]
     ready = scores(*steps[0], 0)
     for k, (head, i) in enumerate(steps):
         now = ready
@@ -290,18 +295,33 @@
             s.sums[head, local:WINDOW] += s.arriving[head, :reach].astype(jnp.float32)
         send_back(head, *pieces[i])
         sends.append((halo(head, *pieces[i]), None))
-    meanwhile()
+    owners = first_owners(n)
+    pick(s.picked_first, s.grads, owners, slice(0, query_cols), rows)
     for head in range(kv_heads):
         for piece in pieces[1:]:
             halo(head, *piece).wait_recv()
-        s.sums[head, WINDOW:] += s.arriving[head, reach:].astype(jnp.float32)
-        for side in range(2):
-            lanes = slice(side * HEAD_SIZE, (side + 1) * HEAD_SIZE)
-            column = query_cols + side * key_cols + head * HEAD_SIZE
-            s.grads[:, column : column + HEAD_SIZE] = s.sums[head, WINDOW:, lanes].astype(
+    columns = [
+        (head, side, query_cols + side * key_cols + head * HEAD_SIZE)
+        for head in range(kv_heads)
+        for side in range(2)
+    ]
+    for head, side, column in columns:
+        lanes = slice(side * HEAD_SIZE, (side + 1) * HEAD_SIZE)
+        for i, owner in enumerate(owners):
+            own = pl.ds(pl.multiple_of(WINDOW + owner * rows, rows), rows)
+            far = pl.ds(pl.multiple_of(reach + owner * rows, rows), rows)
+            value = s.sums[head, own, lanes] + s.arriving[head, far, lanes].astype(jnp.float32)
+            s.picked_first[i * rows : (i + 1) * rows, column : column + HEAD_SIZE] = value.astype(
                 jnp.bfloat16
             )
-    return sends
+
+    def rest():
+        for head, side, column in columns:
+            lanes = slice(side * HEAD_SIZE, (side + 1) * HEAD_SIZE)
+            value = s.sums[head, WINDOW:, lanes] + s.arriving[head, reach:, lanes].astype(jnp.float32)
+            s.grads[:, column : column + HEAD_SIZE] = value.astype(jnp.bfloat16)
+
+    return sends, rest
 
 
 def first_owners(n):
@@ -316,41 +336,25 @@
     return [ring_device(place + step, n) for step in steps + [0]]
 
 
-def pick(target, source, owners, rows, lanes):
+def pick(target, source, owners, lanes, rows):
     for i, owner in enumerate(owners):
         target[i * rows : (i + 1) * rows, lanes] = source[rows_at(owner, rows), lanes]
 
 
-def products(total, picked, s, lanes, piece, add):
+def products(total, picked, s, piece):
     count, width = total.shape[1:]
     for j in range(0, width, TILE):
         at = pl.ds(pl.multiple_of(piece * width + j, TILE), TILE)
-        product = dot(picked[:count, lanes], s.held[at, lanes], 1, 1)
-        if add:
-            product += total[piece, :, j : j + TILE]
-        total[piece, :, j : j + TILE] = product
-
-
-def first_query_sums(n, rows, s):
-    lanes = slice(0, s.query.shape[1])
-    pick(s.picked_first, s.grads, first_owners(n), rows, lanes)
-
-    def piece_sums(piece, carry):
-        products(s.first, s.picked_first, s, lanes, piece, False)
-        return carry
-
-    lax.fori_loop(0, PIECES, piece_sums, 0)
-
-
-def scatter_phase(n, ring, tokens, gain, out, s):
+        total[piece, :, j : j + TILE] = dot(picked[:count], s.held[at], 1, 1)
+
+
+def scatter_phase(n, ring, tokens, gain, out, rest, s):
     rows, width = tokens.shape
     last = n // 2
     half = PIECES // 2
     size = width // PIECES
     cols = s.grads.shape[1]
-    query_cols = s.query.shape[1]
     far = [list(range(half)), list(range(half, PIECES))]
-    orders = [far[1] + far[0], far[0] + far[1]]
 
     def sender(direction, hop, piece):
         return remote(
@@ -361,21 +365,41 @@
             ring[direction],
         )
 
+    def bundle(direction, hop, side):
+        part = pl.ds(side * half, half)
+        return remote(
+            s.outgoing.at[direction, hop - 1, part],
+            s.incoming.at[direction, hop - 1, part],
+            s.scatter_send.at[direction, hop - 1, side * half],
+            s.scatter_recv.at[direction, hop - 1, side * half],
+            ring[direction],
+        )
+
+    def parcels(direction, hop, side):
+        if hop == last or (hop == last - 1 and side != direction):
+            return [sender(direction, hop, piece) for piece in far[side]]
+        return [bundle(direction, hop, side)]
+
     def give(direction, hop, piece, value):
         s.outgoing[direction, hop - 1, piece] = value.astype(jnp.bfloat16)
         sender(direction, hop, piece).start()
 
-    def take(direction, hop, piece):
-        sender(direction, hop, piece).wait_recv()
-        return s.incoming[direction, hop - 1, piece].astype(jnp.float32)
-
-    lanes = slice(query_cols, cols)
-    pick(s.picked_first, s.grads, first_owners(n), rows, lanes)
+    def arrive(direction, hop, side):
+        for copy in parcels(direction, hop, side):
+            copy.wait_recv()
+
+    def relay(direction, hop, side, source, block):
+        arrive(direction, hop + 1, side)
+        for piece in far[side]:
+            value = source[piece, block : block + rows]
+            value += s.incoming[direction, hop, piece].astype(jnp.float32)
+            s.outgoing[direction, hop - 1, piece] = value.astype(jnp.bfloat16)
+        bundle(direction, hop, side).start()
 
     def first_pair(k, carry):
         for direction in range(2):
             piece = direction * half + k
-            products(s.first, s.picked_first, s, lanes, piece, True)
+            products(s.first, s.picked_first, s, piece)
             other = 1 - direction
             block = (1 + other) * rows
             give(direction, last, piece, s.first[piece, :rows])
@@ -384,10 +408,11 @@
 
     lax.fori_loop(0, half, first_pair, 0)
     owners = later_owners(n)
-    pick(s.picked_later, s.grads, owners, rows, slice(0, cols))
+    rest()
+    pick(s.picked_later, s.grads, owners, slice(0, cols), rows)
 
     def later_sums(piece, carry):
-        products(s.later, s.picked_later, s, slice(0, cols), piece, False)
+        products(s.later, s.picked_later, s, piece)
         return carry
 
     lax.fori_loop(0, PIECES, later_sums, 0)
@@ -395,31 +420,27 @@
     scale = lax.rsqrt(jnp.mean(values * values, axis=1, keepdims=True) + EPS)
     s.unit[...] = values * scale
 
-    for k in range(half):
-        for direction in range(2):
-            piece = far[direction][k]
-            block = (1 + direction) * rows
-            value = s.first[piece, block : block + rows]
-            give(direction, last - 1, piece, value + take(direction, last, piece))
+    for direction in range(2):
+        relay(direction, last - 1, direction, s.first, (1 + direction) * rows)
     for hop in range(last - 2, 0, -1):
-        for k in range(PIECES):
+        for turn in range(2):
             for direction in range(2):
-                piece = orders[direction][k]
+                side = direction if turn else 1 - direction
                 block = (2 * (last - 2 - hop) + direction) * rows
-                value = s.later[piece, block : block + rows]
-                give(direction, hop, piece, value + take(direction, hop + 1, piece))
+                relay(direction, hop, side, s.later, block)
     along = jnp.zeros((rows, HEAD_SIZE), jnp.float32)
     block = 2 * (last - 2) * rows
-    done = [set(), set()]
-    for k in range(PIECES):
-        for direction in range(2):
-            done[direction].add(orders[direction][k])
-        for piece in sorted(done[0] & done[1]):
-            for direction in range(2):
-                done[direction].remove(piece)
+    for direction in range(2):
+        side = 1 - direction
+        arrive(direction, 1, side)
+        for piece in far[side]:
+            s.later[piece, block : block + rows] += s.incoming[direction, 0, piece].astype(jnp.float32)
+    for direction in range(2):
+        arrive(direction, 1, direction)
+        for piece in far[direction]:
             at = slice(piece * size, (piece + 1) * size)
             value = s.later[piece, block : block + rows]
-            value = value + take(0, 1, piece) + take(1, 1, piece)
+            value += s.incoming[direction, 0, piece].astype(jnp.float32)
             upper = value * gain[:, at]
             s.upper[:, at] = upper
             product = upper * s.unit[:, at]
@@ -430,10 +451,12 @@
         at = slice(piece * size, (piece + 1) * size)
         out[:, at] = (scale * (s.upper[:, at] - s.unit[:, at] * mean)).astype(jnp.bfloat16)
     return [
-        sender(direction, hop, piece)
+        copy
         for hop in range(last, 0, -1)
         for direction in range(2)
-        for piece in (far[direction] if hop == last else orders[direction])
+        for side in range(2)
+        if hop < last or side == direction
+        for copy in parcels(direction, hop, side)
     ]
 
 
@@ -455,9 +478,9 @@
     load.wait()
     hear(ring + onward + backward)
     sends = gather_phase(n, ring, onward, tokens, s.gain, loads, s)
-    meanwhile = functools.partial(first_query_sums, n, tokens.shape[0], s)
-    sends += attention_phase(backward[0], s.output_grad, s, meanwhile)
-    sends += [(copy, None) for copy in scatter_phase(n, ring, tokens, s.gain, out, s)]
+    halos, rest = attention_phase(n, tokens.shape[0], backward[0], s.output_grad, s)
+    sends += halos
+    sends += [(copy, None) for copy in scatter_phase(n, ring, tokens, s.gain, out, rest, s)]
     for copy, needed in sends:
         when(needed, copy.wait_send)
 

time: 114 us -> 112 us (0.982)
  Pallas kernels: 113 us -> 111 us
    pallas_call x1, Pallas kernels: 113 us -> 111 us  [on_device(): pl.pallas_call(functools.partial(kernel, tuple(scratch), n, lax.axis_size...]
where the time goes in v3:
time: 112 us
  Pallas kernels  111 us (99%)
    pallas_call x1, Pallas kernels, on_device(): pl.pallas_call(functools.partial(kernel, tuple(scratch), n, lax.axis_size...  111 us

profile of v3, /device:TPU:1, one launch (start us, length us, event | category | flops | bytes accessed | tf_op | source)
XLA Modules:
  0.0 111.7 jit_solution(15255296833653574282)
XLA Ops:
  0.0 110.9 %attention_backward.1 = bf16[64,4608]{1,0:T(8,128)(2,1)S(1)} custom-call(bf16[64,4608]{1,0:T(8,128)(2,1)} %tokens_ref.1, f32[4608]{0:T(1024)} %gain_ref.1, bf16[512,512]{1,0:T(8,128)(2,1)} %grad_ref.1, bf16[4608,512]{1,0:T(8,128)(2,1)} %wq.1, bf16[4608,256]{1,0:T(8,128)(2,1)} %wk.1, bf16[4608,256]{1,0:T(8,128)(2,1)} %wv.1), custom_call_target="tpu_custom_call" | custom-call | tf_op jit(solution)/shard_map/attention_backward/pallas_call | solution.py:539
  110.9 0.8 copy.8

commit v4 on v3

--- a/solution.py
+++ b/solution.py
@@ -88,6 +88,7 @@
     rows, _ = tokens.shape
     local = n * rows
     half = rows // 2
+    quarter = half // 2
     last = n // 2
     query_cols = s.query.shape[1]
     pair_cols = s.pairs.shape[1]
@@ -108,43 +109,65 @@
             ring[direction],
         )
 
-    def project(sources):
-        for i, (block, _) in enumerate(sources):
+    def last_sender(direction, stage):
+        owner = ring_device(place + (1 - last if direction == 0 else last - 1), n)
+        part = pl.ds(direction * half + stage * quarter, quarter)
+        return remote(
+            s.gathered.at[owner, part],
+            s.gathered.at[owner, part],
+            s.gather_send.at[direction, last - 1, stage],
+            s.gather_recv.at[direction, last - 1, stage],
+            ring[direction],
+        )
+
+    def normalize(pieces, at):
+        for block, _, size in pieces:
             values = block[...].astype(jnp.float32)
             scale = lax.rsqrt(jnp.mean(values * values, axis=1, keepdims=True) + EPS)
-            s.normed[i * rows : (i + 1) * rows] = (values * scale * gain[...]).astype(jnp.bfloat16)
-        count = len(sources) * rows
-
-        def column(target, base, first):
-            def write(j, carry):
-                product = jnp.dot(
-                    s.normed[:count],
-                    s.held[:, pl.ds(pl.multiple_of(first + j * TILE, TILE), TILE)],
-                    preferred_element_type=jnp.float32,
-                ).astype(jnp.bfloat16)
-                for i, (_, owner) in enumerate(sources):
-                    at = pl.ds(pl.multiple_of(base + owner * rows, rows), rows)
-                    target[at, rows_at(j, TILE)] = product[i * rows : (i + 1) * rows]
-                return carry
-
-            return write
-
-        lax.fori_loop(0, pair_cols // TILE, column(s.pairs, 2 * local, query_cols), 0)
-        for _, owner in sources:
+            s.normed[at : at + size] = (values * scale * gain[...]).astype(jnp.bfloat16)
+            at += size
+
+    def columns(pieces, at, tiles, target, base, first):
+        count = sum(size for _, _, size in pieces)
+
+        def write(j, carry):
+            product = jnp.dot(
+                s.normed[at : at + count],
+                s.held[:, pl.ds(pl.multiple_of(first + j * TILE, TILE), TILE)],
+                preferred_element_type=jnp.float32,
+            ).astype(jnp.bfloat16)
+            done = 0
+            for _, row, size in pieces:
+                to = pl.ds(pl.multiple_of(base + row, size), size)
+                target[to, rows_at(j, TILE)] = product[done : done + size]
+                done += size
+            return carry
+
+        lax.fori_loop(0, tiles, write, 0)
+
+    def pairs(pieces, at):
+        columns(pieces, at, pair_cols // TILE, s.pairs, 2 * local, query_cols)
+        for _, row, size in pieces:
             for back in range(2):
-                source = pl.ds(pl.multiple_of(2 * local + owner * rows, rows), rows)
-                target = pl.ds(pl.multiple_of((1 - back) * local + owner * rows, rows), rows)
                 copy = remote(
-                    s.pairs.at[source],
-                    s.pairs.at[target],
+                    s.pairs.at[pl.ds(pl.multiple_of(2 * local + row, size), size)],
+                    s.pairs.at[pl.ds(pl.multiple_of((1 - back) * local + row, size), size)],
                     s.halo_send.at[back, len(halos) // 2],
                     s.halo_recv.at[back, len(halos) // 2],
                     onward[back],
                 )
-                needed = (owner + 1) * rows > 2 * local - WINDOW if back else None
+                needed = row + size > 2 * local - WINDOW if back else None
                 halos.append((copy, needed))
                 when(needed, copy.start)
-        lax.fori_loop(0, query_cols // TILE, column(s.query, 0, 0), 0)
+
+    def queries(pieces, at):
+        columns(pieces, at, query_cols // TILE, s.query, 0, 0)
+
+    def project(sources):
+        pieces = [(block, owner * rows, rows) for block, owner in sources]
+        normalize(pieces, 0)
+        pairs(pieces, 0)
+        queries(pieces, 0)
 
     for position in range(2):
         for direction in range(2):
@@ -157,20 +180,31 @@
     gain[...] = s.gain_flat[...].reshape(gain.shape)
     project([(tokens, me)])
     prepare_attention(s)
-    for hop in range(1, last + 1):
+    for hop in range(1, last):
         for position in range(2):
             for direction in range(2):
-                order = chunks_of(direction, hop, last)
-                if position < len(order):
-                    chunk = order[position]
-                    sender(direction, hop, chunk).wait_recv()
-                    if hop < last and chunk in chunks_of(direction, hop + 1, last):
-                        sends.append(sender(direction, hop + 1, chunk))
+                chunk = chunks_of(direction, hop, last)[position]
+                sender(direction, hop, chunk).wait_recv()
+                if hop + 1 < last:
+                    sends.append(sender(direction, hop + 1, chunk))
+                    sends[-1].start()
+                elif chunk == direction:
+                    for stage in range(2):
+                        sends.append(last_sender(direction, stage))
                         sends[-1].start()
-        owners = [ring_device(place - hop, n)]
-        if hop < last:
-            owners.append(ring_device(place + hop, n))
+        owners = [ring_device(place - hop, n), ring_device(place + hop, n)]
         project([(s.gathered.at[owner], owner) for owner in owners])
+    owner = ring_device(place + last, n)
+    pieces = []
+    for stage in range(2):
+        for direction in range(2):
+            last_sender(direction, stage).wait_recv()
+            first = direction * half + stage * quarter
+            block = s.gathered.at[owner, first : first + quarter]
+            pieces.append((block, owner * rows + first, quarter))
+        normalize(pieces[2 * stage :], stage * half)
+        pairs(pieces[2 * stage :], stage * half)
+    queries(pieces, 0)
     for copy, needed in halos:
         when(needed, copy.wait_recv)
     return [(copy, None) for copy in sends] + halos
@@ -496,7 +530,7 @@
     low, full = jnp.bfloat16, jnp.float32
     hops = pltpu.SemaphoreType.DMA((2, n // 2, 2))
     pieces = pltpu.SemaphoreType.DMA((2, n // 2, PIECES))
-    blocks = pltpu.SemaphoreType.DMA((2, n))
+    blocks = pltpu.SemaphoreType.DMA((2, n + 3))
     heads = pltpu.SemaphoreType.DMA((kv_heads, local // QUERY_ROWS))
     scratch = dict(
         tokens=pltpu.VMEM((rows, width), low),

time: 112 us -> 111 us (level)
  no operation moved by 1% of the time
where the time goes in v4:
time: 111 us
  Pallas kernels  110 us (99%)
    pallas_call x1, Pallas kernels, on_device(): pl.pallas_call(functools.partial(kernel, tuple(scratch), n, lax.axis_size...  110 us

profile of v4, /device:TPU:1, one launch (start us, length us, event | category | flops | bytes accessed | tf_op | source)
XLA Modules:
  0.0 111.2 jit_solution(14320661821463652718)
XLA Ops:
  0.0 110.4 %attention_backward.1 = bf16[64,4608]{1,0:T(8,128)(2,1)S(1)} custom-call(bf16[64,4608]{1,0:T(8,128)(2,1)} %tokens_ref.1, f32[4608]{0:T(1024)} %gain_ref.1, bf16[512,512]{1,0:T(8,128)(2,1)} %grad_ref.1, bf16[4608,512]{1,0:T(8,128)(2,1)} %wq.1, bf16[4608,256]{1,0:T(8,128)(2,1)} %wk.1, bf16[4608,256]{1,0:T(8,128)(2,1)} %wv.1), custom_call_target="tpu_custom_call" | custom-call | tf_op jit(solution)/shard_map/attention_backward/pallas_call | solution.py:573
  110.4 0.8 copy.8

commit v5 on v4

--- a/solution.py
+++ b/solution.py
@@ -410,7 +410,8 @@
         )
 
     def parcels(direction, hop, side):
-        if hop == last or (hop == last - 1 and side != direction):
+        single = (hop == 1) if side == direction else (hop == last - 1)
+        if hop == last or single:
             return [sender(direction, hop, piece) for piece in far[side]]
         return [bundle(direction, hop, side)]
 
@@ -428,7 +429,8 @@
             value = source[piece, block : block + rows]
             value += s.incoming[direction, hop, piece].astype(jnp.float32)
             s.outgoing[direction, hop - 1, piece] = value.astype(jnp.bfloat16)
-        bundle(direction, hop, side).start()
+        for copy in parcels(direction, hop, side):
+            copy.start()
 
     def first_pair(k, carry):
         for direction in range(2):
@@ -469,9 +471,10 @@
         arrive(direction, 1, side)
         for piece in far[side]:
             s.later[piece, block : block + rows] += s.incoming[direction, 0, piece].astype(jnp.float32)
-    for direction in range(2):
-        arrive(direction, 1, direction)
-        for piece in far[direction]:
+    for k in range(half):
+        for direction in range(2):
+            piece = far[direction][k]
+            sender(direction, 1, piece).wait_recv()
             at = slice(piece * size, (piece + 1) * size)
             value = s.later[piece, block : block + rows]
             value += s.incoming[direction, 0, piece].astype(jnp.float32)

time: 111 us -> 111 us (level)
  no operation moved by 1% of the time
where the time goes in v5:
time: 111 us
  Pallas kernels  110 us (99%)
    pallas_call x1, Pallas kernels, on_device(): pl.pallas_call(functools.partial(kernel, tuple(scratch), n, lax.axis_size...  110 us

profile of v5, /device:TPU:1, one launch (start us, length us, event | category | flops | bytes accessed | tf_op | source)
XLA Modules:
  0.0 111.1 jit_solution(3674419935841650819)
XLA Ops:
  0.0 110.3 %attention_backward.1 = bf16[64,4608]{1,0:T(8,128)(2,1)S(1)} custom-call(bf16[64,4608]{1,0:T(8,128)(2,1)} %tokens_ref.1, f32[4608]{0:T(1024)} %gain_ref.1, bf16[512,512]{1,0:T(8,128)(2,1)} %grad_ref.1, bf16[4608,512]{1,0:T(8,128)(2,1)} %wq.1, bf16[4608,256]{1,0:T(8,128)(2,1)} %wk.1, bf16[4608,256]{1,0:T(8,128)(2,1)} %wv.1), custom_call_target="tpu_custom_call" | custom-call | tf_op jit(solution)/shard_map/attention_backward/pallas_call | solution.py:576
  110.3 0.8 copy.8
